TPU v7x, 8 devices: a whole 2x2x1 slice. The times are simulated.
8 devices in a mesh: dp: 2 (over z, y), sp: 4 (over x, core).
Axes of the slice: x: 2, y: 2, z: 1, core: 2. Of those that a mesh axis runs over, the one named last changes fastest.
Arguments:
- hidden_states: bfloat16 [12, 384, 2304], P('dp', 'sp'), parts along dimension 0
- positions: int32 [12, 384], P('dp', 'sp'), parts along dimension 0
- gain_attn: float32 [8, 2304], replicated
- gain_mlp: float32 [8, 2304], replicated
- w_query: bfloat16 [8, 2304, 8, 256], replicated
- w_key: bfloat16 [8, 2304, 4, 256], replicated
- w_value: bfloat16 [8, 2304, 4, 256], replicated
- w_out: bfloat16 [8, 8, 256, 2304], replicated
- w_gate: bfloat16 [8, 2304, 9216], replicated
- w_up: bfloat16 [8, 2304, 9216], replicated
- w_down: bfloat16 [8, 9216, 2304], replicated
Outputs:
- output: bfloat16 [12, 384, 2304], P('dp', 'sp'), parts along dimension 0
There are 2 independent parts. A program takes and returns all parts, laid end to end along the dimension named above; an argument that names none is the same for every part.
All inputs are finite; a program needn't handle non-finite values.
Results may differ from a plain program's by a relative error of at most 0.0175564.
Values are sent between devices in bfloat16 or wider.
A program may use at most 4.75 GiB of HBM per device.

v0:
```python
import jax
import jax.numpy as jnp
from jax import lax
from jax.sharding import PartitionSpec as P

EPSILON = 1e-5
THETA = 10000.0


def rms_norm(values, gain):
    as_float = values.astype(jnp.float32)
    inv_rms = lax.rsqrt(jnp.mean(as_float * as_float, axis=-1, keepdims=True) + EPSILON)
    return (as_float * inv_rms * gain).astype(jnp.bfloat16)


def rotary(values, cos_t, sin_t):
    half_dim = values.shape[-1] // 2
    lower_part = values[..., :half_dim]
    upper_part = values[..., half_dim:]
    return jnp.concatenate([lower_part * cos_t - upper_part * sin_t, upper_part * cos_t + lower_part * sin_t], axis=-1)


def rope_tables(positions, head_dim):
    half_dim = head_dim // 2
    inv_freq = THETA ** (-(jnp.arange(half_dim, dtype=jnp.float32) * 2.0) / head_dim)
    angles = positions.astype(jnp.float32)[:, :, None] * inv_freq
    return jnp.cos(angles)[:, :, None, :], jnp.sin(angles)[:, :, None, :]


def project_qkv(hidden, gain, q_weight, k_weight, v_weight, cos_t, sin_t):
    normed = rms_norm(hidden, gain)
    queries = jnp.einsum('btd,dhe->bthe', normed, q_weight, preferred_element_type=jnp.float32)
    keys = jnp.einsum('btd,dhe->bthe', normed, k_weight, preferred_element_type=jnp.float32)
    values = jnp.einsum('btd,dhe->bthe', normed, v_weight, preferred_element_type=jnp.float32)
    return rotary(queries, cos_t, sin_t).astype(jnp.bfloat16), rotary(keys, cos_t, sin_t).astype(jnp.bfloat16), values.astype(jnp.bfloat16)


def attend(query_groups, keys_ctx, values_ctx, valid):
    head_dim = query_groups.shape[-1]
    scores = jnp.einsum('bqhgd,bkhd->bhgqk', query_groups, keys_ctx, preferred_element_type=jnp.float32) * head_dim ** -0.5
    scores = jnp.where(valid, scores, -jnp.inf)
    attn_probs = jax.nn.softmax(scores, axis=-1).astype(jnp.bfloat16)
    attn_vals = jnp.einsum('bhgqk,bkhd->bqhgd', attn_probs, values_ctx, preferred_element_type=jnp.float32).astype(jnp.bfloat16)
    return attn_vals.reshape(attn_vals.shape[0], attn_vals.shape[1], -1, head_dim)


def mlp_block(hidden, gain, gate_weight, up_weight, down_weight):
    normed = rms_norm(hidden, gain)
    gate_proj = jnp.einsum('btd,df->btf', normed, gate_weight, preferred_element_type=jnp.float32)
    up_proj = jnp.einsum('btd,df->btf', normed, up_weight, preferred_element_type=jnp.float32)
    activated = (jax.nn.silu(gate_proj) * up_proj).astype(jnp.bfloat16)
    down_proj = jnp.einsum('btf,fd->btd', activated, down_weight, preferred_element_type=jnp.float32)
    return (hidden.astype(jnp.float32) + down_proj).astype(jnp.bfloat16)


def solution(mesh):
    n_seq = mesh.shape['sp']
    shift_one = [(source, source + 1) for source in range(n_seq - 1)]
    shift_two = [(source, source + 2) for source in range(n_seq - 2)]

    def local_stack(hidden_states, positions, gain_attn, gain_mlp, w_query, w_key, w_value, w_out, w_gate, w_up, w_down):
        batch, seq_dev, _ = hidden_states.shape
        kv_heads, head_dim = w_key.shape[2], w_key.shape[3]
        group_size = w_query.shape[2] // kv_heads
        tail_len = seq_dev // 2
        halo_len = seq_dev + tail_len
        window = 3 * seq_dev // 2
        cos_t, sin_t = rope_tables(positions, head_dim)
        shard = lax.axis_index('sp')
        q_index = jnp.arange(seq_dev)[:, None]
        k_index = jnp.arange(halo_len + seq_dev)[None, :]
        distance = q_index + halo_len - k_index
        valid = (distance >= 0) & (distance < window) & (k_index >= halo_len - shard * seq_dev)
        hidden = hidden_states
        for layer in range(w_query.shape[0]):
            queries, keys, values = project_qkv(hidden, gain_attn[layer], w_query[layer], w_key[layer], w_value[layer], cos_t, sin_t)
            left_keys, left_values = lax.ppermute((keys, values), 'sp', shift_one)
            far_keys, far_values = lax.ppermute((keys[:, seq_dev - tail_len:], values[:, seq_dev - tail_len:]), 'sp', shift_two)
            keys_ctx = jnp.concatenate([far_keys, left_keys, keys], axis=1)
            values_ctx = jnp.concatenate([far_values, left_values, values], axis=1)
            query_groups = queries.reshape(batch, seq_dev, kv_heads, group_size, head_dim)
            attn_vals = attend(query_groups, keys_ctx, values_ctx, valid)
            attn_proj = jnp.einsum('bthe,hed->btd', attn_vals, w_out[layer], preferred_element_type=jnp.float32)
            hidden = (hidden.astype(jnp.float32) + attn_proj).astype(jnp.bfloat16)
            hidden = mlp_block(hidden, gain_mlp[layer], w_gate[layer], w_up[layer], w_down[layer])
        return hidden

    row_spec = P('dp', 'sp', None)
    return jax.shard_map(local_stack, mesh=mesh, in_specs=(row_spec, P('dp', 'sp'), P(), P(), P(), P(), P(), P(), P(), P(), P()), out_specs=row_spec, check_vma=False)
```

profile of v0, /device:TPU:1, one launch (start us, length us, event | category | flops | bytes accessed | tf_op | source)
XLA Modules:
  0.0 1527.2 jit_solution(8450386819024042316)
XLA Ops:
  5.4 29.2 %fusion.590 = (bf16[1,2304,4,256]{3,2,1,0:T(4,128)(2,1)}, bf16[1,2304,4,256]{3,2,1,0:T(4,128)(2,1)}, bf16[1,2304,4,256]{3,2,1,0:T(4,128)(2,1)}, bf16[1,2304,4,25...) fusion(bf16[8,2304,4,256]{3,2,1,0:T(4,128)(2,1)} %param.16), kind=kLoop, calls=%fused_computation.668 | loop fusion | bytes 75497472 | tf_op jit(solution)/shard_map/slice | solution.py:76
  46.6 29.1 %fusion.589 = (bf16[1,2304,4,256]{3,2,1,0:T(4,128)(2,1)}, bf16[1,2304,4,256]{3,2,1,0:T(4,128)(2,1)}, bf16[1,2304,4,256]{3,2,1,0:T(4,128)(2,1)}, bf16[1,2304,4,25...) fusion(bf16[8,2304,4,256]{3,2,1,0:T(4,128)(2,1)} %param.17), kind=kLoop, calls=%fused_computation.667 | loop fusion | bytes 75497472 | tf_op jit(solution)/shard_map/slice | solution.py:76
  85.7 49.1 %fusion.588 = (bf16[1,2304,8,256]{3,2,1,0:T(8,128)(2,1)}, bf16[1,2304,8,256]{3,2,1,0:T(8,128)(2,1)}, bf16[1,2304,8,256]{3,2,1,0:T(8,128)(2,1)}, bf16[1,2304,8,25...) fusion(bf16[8,2304,8,256]{3,2,1,0:T(8,128)(2,1)} %param.15), kind=kLoop, calls=%fused_computation.666 | loop fusion | bytes 150994944 | tf_op jit(solution)/shard_map/slice | solution.py:76
  158.4 10.9 fusion.156
  169.3 33.1 %fusion.54 = f32[6,96,9216]{2,1,0:T(8,128)} fusion(bf16[8,2304,9216]{2,1,0:T(8,128)(2,1)} %param.19, bf16[6,96,2304]{2,1,0:T(8,128)(2,1)} %get-tuple-element.82, f32[2304]{0:T(1024)S(1)} %get-tuple-element.11, f32[6,96]{1,0:T(8,128)S(1)} %add_rsqrt_fusion.14), kind=kOutput, calls=%fused_computation.54 | convolution fusion | flops 24466489344 | bytes 66366720 | tf_op jit(solution)/shard_map/btd,df->btf/dot_general | solution.py:49
  202.4 34.3 %multiply_convert_fusion.7.clone.3.clone.5 = bf16[6,96,9216]{2,1,0:T(8,128)(2,1)} fusion(f32[6,96,9216]{2,1,0:T(8,128)} %fusion.54, bf16[8,2304,9216]{2,1,0:T(8,128)(2,1)} %param.20, bf16[6,96,2304]{2,1,0:T(8,128)(2,1)} %get-tuple-element.82, f32[2304]{0:T(1024)S(1)} %get-tuple-element.11, ...), kind=kOutput, calls=%fused_computation.87.clone.clone.clone.clone.clone.clone.clone.2 | convolution fusion | flops 24498339840 | bytes 76983552 | tf_op jit(solution)/shard_map/btd,df->btf/dot_general | solution.py:50
  236.6 34.2 %fusion.160 = (f32[6,96]{1,0:T(8,128)S(1)}, bf16[6,96,2304]{2,1,0:T(8,128)(2,1)S(1)}) fusion(bf16[8,9216,2304]{2,1,0:T(8,128)(2,1)} %param.21, bf16[6,96,2304]{2,1,0:T(8,128)(2,1)} %get-tuple-element.82, bf16[6,96,9216]{2,1,0:T(8,128)(2,1)} %multiply_convert_fusion.7.clone.3.clone.5), kind=kOutput, calls=%fused_computation.192 | convolution fusion | flops 24469143552 | bytes 58394880 | tf_op jit(solution)/shard_map/btf,fd->btd/dot_general | solution.py:52
  293.3 23.5 %collective-permute-done.6 = bf16[6,48,4,256]{3,1,2,0:T(8,128)(2,1)S(1)} collective-permute-done((bf16[6,48,4,256]{3,1,2,0:T(8,128)(2,1)S(1)}, bf16[6,48,4,256]{3,1,2,0:T(8,128)(2,1)S(1)}, u32[]{:S(2)}, u32[]{:S(2)}) %collective-permute-start.6) | collective-permute-done | bytes 589856 | tf_op jit(solution)/shard_map/ppermute | solution.py:78
  320.9 14.9 collective-permute-done.4
  337.2 10.8 fusion.164
  348.0 32.8 %fusion.48 = f32[6,96,9216]{2,1,0:T(8,128)} fusion(bf16[8,2304,9216]{2,1,0:T(8,128)(2,1)} %param.19, bf16[6,96,2304]{2,1,0:T(8,128)(2,1)} %get-tuple-element.88, f32[2304]{0:T(1024)S(1)} %copy-done.30, f32[6,96]{1,0:T(8,128)S(1)} %add_rsqrt_fusion.12), kind=kOutput, calls=%fused_computation.48 | convolution fusion | flops 24466489344 | bytes 66366720 | tf_op jit(solution)/shard_map/btd,df->btf/dot_general | solution.py:49
  380.8 34.5 %multiply_convert_fusion.6.clone.3.clone.5 = bf16[6,96,9216]{2,1,0:T(8,128)(2,1)} fusion(f32[6,96,9216]{2,1,0:T(8,128)} %fusion.48, bf16[8,2304,9216]{2,1,0:T(8,128)(2,1)} %param.20, bf16[6,96,2304]{2,1,0:T(8,128)(2,1)} %get-tuple-element.88, f32[2304]{0:T(1024)S(1)} %copy-done.30, f32[6,96]{1,0:T(8,128)S(1)} %add_rsqrt_fusion.12), kind=kOutput, calls=%fused_computation.86.clone.clone.clone.clone.clone.clone.clone.2 | convolution fusion | flops 24498339840 | bytes 76983552 | tf_op jit(solution)/shard_map/btd,df->btf/dot_general | solution.py:50
  415.3 34.1 %fusion.168 = (f32[6,96]{1,0:T(8,128)S(1)}, bf16[6,96,2304]{2,1,0:T(8,128)(2,1)S(1)}) fusion(bf16[8,9216,2304]{2,1,0:T(8,128)(2,1)} %param.21, bf16[6,96,2304]{2,1,0:T(8,128)(2,1)} %get-tuple-element.88, bf16[6,96,9216]{2,1,0:T(8,128)(2,1)} %multiply_convert_fusion.6.clone.3.clone.5), kind=kOutput, calls=%fused_computation.200 | convolution fusion | flops 24469143552 | bytes 58394880 | tf_op jit(solution)/shard_map/btf,fd->btd/dot_general | solution.py:52
  474.3 21.4 %collective-permute-done.10 = bf16[6,48,4,256]{3,1,2,0:T(8,128)(2,1)S(1)} collective-permute-done((bf16[6,48,4,256]{3,1,2,0:T(8,128)(2,1)S(1)}, bf16[6,48,4,256]{3,1,2,0:T(8,128)(2,1)S(1)}, u32[]{:S(2)}, u32[]{:S(2)}) %collective-permute-start.10) | collective-permute-done | bytes 589856 | tf_op jit(solution)/shard_map/ppermute | solution.py:78
  500.0 14.7 collective-permute-done.8
  516.1 10.8 fusion.172
  526.9 32.7 %fusion.42 = f32[6,96,9216]{2,1,0:T(8,128)} fusion(bf16[8,2304,9216]{2,1,0:T(8,128)(2,1)} %param.19, bf16[6,96,2304]{2,1,0:T(8,128)(2,1)} %get-tuple-element.94, f32[2304]{0:T(1024)S(1)} %copy-done.28, f32[6,96]{1,0:T(8,128)S(1)} %add_rsqrt_fusion.10), kind=kOutput, calls=%fused_computation.42 | convolution fusion | flops 24466489344 | bytes 66366720 | tf_op jit(solution)/shard_map/btd,df->btf/dot_general | solution.py:49
  559.7 34.4 %multiply_convert_fusion.5.clone.3.clone.5 = bf16[6,96,9216]{2,1,0:T(8,128)(2,1)} fusion(f32[6,96,9216]{2,1,0:T(8,128)} %fusion.42, bf16[8,2304,9216]{2,1,0:T(8,128)(2,1)} %param.20, bf16[6,96,2304]{2,1,0:T(8,128)(2,1)} %get-tuple-element.94, f32[2304]{0:T(1024)S(1)} %copy-done.28, f32[6,96]{1,0:T(8,128)S(1)} %add_rsqrt_fusion.10), kind=kOutput, calls=%fused_computation.85.clone.clone.clone.clone.clone.clone.clone.2 | convolution fusion | flops 24498339840 | bytes 76983552 | tf_op jit(solution)/shard_map/btd,df->btf/dot_general | solution.py:50
  594.1 34.0 %fusion.176 = (f32[6,96]{1,0:T(8,128)S(1)}, bf16[6,96,2304]{2,1,0:T(8,128)(2,1)S(1)}) fusion(bf16[8,9216,2304]{2,1,0:T(8,128)(2,1)} %param.21, bf16[6,96,2304]{2,1,0:T(8,128)(2,1)} %get-tuple-element.94, bf16[6,96,9216]{2,1,0:T(8,128)(2,1)} %multiply_convert_fusion.5.clone.3.clone.5), kind=kOutput, calls=%fused_computation.208 | convolution fusion | flops 24469143552 | bytes 58394880 | tf_op jit(solution)/shard_map/btf,fd->btd/dot_general | solution.py:52
  653.2 21.4 %collective-permute-done.14 = bf16[6,48,4,256]{3,1,2,0:T(8,128)(2,1)S(1)} collective-permute-done((bf16[6,48,4,256]{3,1,2,0:T(8,128)(2,1)S(1)}, bf16[6,48,4,256]{3,1,2,0:T(8,128)(2,1)S(1)}, u32[]{:S(2)}, u32[]{:S(2)}) %collective-permute-start.14) | collective-permute-done | bytes 589856 | tf_op jit(solution)/shard_map/ppermute | solution.py:78
  678.8 14.7 collective-permute-done.12
  694.9 10.8 fusion.180
  705.8 33.0 %fusion.36 = f32[6,96,9216]{2,1,0:T(8,128)} fusion(bf16[8,2304,9216]{2,1,0:T(8,128)(2,1)} %param.19, bf16[6,96,2304]{2,1,0:T(8,128)(2,1)} %get-tuple-element.100, f32[2304]{0:T(1024)S(1)} %copy-done.26, f32[6,96]{1,0:T(8,128)S(1)} %add_rsqrt_fusion.8), kind=kOutput, calls=%fused_computation.36 | convolution fusion | flops 24466489344 | bytes 66366720 | tf_op jit(solution)/shard_map/btd,df->btf/dot_general | solution.py:49
  738.7 34.5 %multiply_convert_fusion.4.clone.3.clone.5 = bf16[6,96,9216]{2,1,0:T(8,128)(2,1)} fusion(f32[6,96,9216]{2,1,0:T(8,128)} %fusion.36, bf16[8,2304,9216]{2,1,0:T(8,128)(2,1)} %param.20, bf16[6,96,2304]{2,1,0:T(8,128)(2,1)} %get-tuple-element.100, f32[2304]{0:T(1024)S(1)} %copy-done.26, f32[6,96]{1,0:T(8,128)S(1)} %add_rsqrt_fusion.8), kind=kOutput, calls=%fused_computation.84.clone.clone.clone.clone.clone.clone.clone.2 | convolution fusion | flops 24498339840 | bytes 76983552 | tf_op jit(solution)/shard_map/btd,df->btf/dot_general | solution.py:50
  773.2 33.9 %fusion.184 = (f32[6,96]{1,0:T(8,128)S(1)}, bf16[6,96,2304]{2,1,0:T(8,128)(2,1)S(1)}) fusion(bf16[8,9216,2304]{2,1,0:T(8,128)(2,1)} %param.21, bf16[6,96,2304]{2,1,0:T(8,128)(2,1)} %get-tuple-element.100, bf16[6,96,9216]{2,1,0:T(8,128)(2,1)} %multiply_convert_fusion.4.clone.3.clone.5), kind=kOutput, calls=%fused_computation.216 | convolution fusion | flops 24469143552 | bytes 58394880 | tf_op jit(solution)/shard_map/btf,fd->btd/dot_general | solution.py:52
  832.2 21.4 %collective-permute-done.18 = bf16[6,48,4,256]{3,1,2,0:T(8,128)(2,1)S(1)} collective-permute-done((bf16[6,48,4,256]{3,1,2,0:T(8,128)(2,1)S(1)}, bf16[6,48,4,256]{3,1,2,0:T(8,128)(2,1)S(1)}, u32[]{:S(2)}, u32[]{:S(2)}) %collective-permute-start.18) | collective-permute-done | bytes 589856 | tf_op jit(solution)/shard_map/ppermute | solution.py:78
  857.8 14.7 collective-permute-done.16
  873.9 10.8 fusion.188
  884.8 32.7 %fusion.30 = f32[6,96,9216]{2,1,0:T(8,128)} fusion(bf16[8,2304,9216]{2,1,0:T(8,128)(2,1)} %param.19, bf16[6,96,2304]{2,1,0:T(8,128)(2,1)} %get-tuple-element.106, f32[2304]{0:T(1024)S(1)} %copy-done.24, f32[6,96]{1,0:T(8,128)S(1)} %add_rsqrt_fusion.6), kind=kOutput, calls=%fused_computation.30 | convolution fusion | flops 24466489344 | bytes 66366720 | tf_op jit(solution)/shard_map/btd,df->btf/dot_general | solution.py:49
  917.4 34.6 %multiply_convert_fusion.3.clone.3.clone.5 = bf16[6,96,9216]{2,1,0:T(8,128)(2,1)} fusion(f32[6,96,9216]{2,1,0:T(8,128)} %fusion.30, bf16[8,2304,9216]{2,1,0:T(8,128)(2,1)} %param.20, bf16[6,96,2304]{2,1,0:T(8,128)(2,1)} %get-tuple-element.106, f32[2304]{0:T(1024)S(1)} %copy-done.24, f32[6,96]{1,0:T(8,128)S(1)} %add_rsqrt_fusion.6), kind=kOutput, calls=%fused_computation.83.clone.clone.clone.clone.clone.clone.clone.2 | convolution fusion | flops 24498339840 | bytes 76983552 | tf_op jit(solution)/shard_map/btd,df->btf/dot_general | solution.py:50
  952.0 34.0 %fusion.192 = (f32[6,96]{1,0:T(8,128)S(1)}, bf16[6,96,2304]{2,1,0:T(8,128)(2,1)S(1)}) fusion(bf16[8,9216,2304]{2,1,0:T(8,128)(2,1)} %param.21, bf16[6,96,2304]{2,1,0:T(8,128)(2,1)} %get-tuple-element.106, bf16[6,96,9216]{2,1,0:T(8,128)(2,1)} %multiply_convert_fusion.3.clone.3.clone.5), kind=kOutput, calls=%fused_computation.224 | convolution fusion | flops 24469143552 | bytes 58394880 | tf_op jit(solution)/shard_map/btf,fd->btd/dot_general | solution.py:52
  1011.0 21.4 %collective-permute-done.22 = bf16[6,48,4,256]{3,1,2,0:T(8,128)(2,1)S(1)} collective-permute-done((bf16[6,48,4,256]{3,1,2,0:T(8,128)(2,1)S(1)}, bf16[6,48,4,256]{3,1,2,0:T(8,128)(2,1)S(1)}, u32[]{:S(2)}, u32[]{:S(2)}) %collective-permute-start.22) | collective-permute-done | bytes 589856 | tf_op jit(solution)/shard_map/ppermute | solution.py:78
  1036.7 14.7 collective-permute-done.20
  1063.6 32.7 %fusion.24 = f32[6,96,9216]{2,1,0:T(8,128)} fusion(bf16[8,2304,9216]{2,1,0:T(8,128)(2,1)} %param.19, bf16[6,96,2304]{2,1,0:T(8,128)(2,1)} %get-tuple-element.112, f32[2304]{0:T(1024)S(1)} %copy-done.22, f32[6,96]{1,0:T(8,128)S(1)} %add_rsqrt_fusion.4), kind=kOutput, calls=%fused_computation.24 | convolution fusion | flops 24466489344 | bytes 66366720 | tf_op jit(solution)/shard_map/btd,df->btf/dot_general | solution.py:49
  1096.3 34.4 %multiply_convert_fusion.2.clone.3.clone.5 = bf16[6,96,9216]{2,1,0:T(8,128)(2,1)} fusion(f32[6,96,9216]{2,1,0:T(8,128)} %fusion.24, bf16[8,2304,9216]{2,1,0:T(8,128)(2,1)} %param.20, bf16[6,96,2304]{2,1,0:T(8,128)(2,1)} %get-tuple-element.112, f32[2304]{0:T(1024)S(1)} %copy-done.22, f32[6,96]{1,0:T(8,128)S(1)} %add_rsqrt_fusion.4), kind=kOutput, calls=%fused_computation.82.clone.clone.clone.clone.clone.clone.clone.2 | convolution fusion | flops 24498339840 | bytes 76983552 | tf_op jit(solution)/shard_map/btd,df->btf/dot_general | solution.py:50
  1130.7 34.1 %fusion.200 = (f32[6,96]{1,0:T(8,128)S(1)}, bf16[6,96,2304]{2,1,0:T(8,128)(2,1)S(1)}) fusion(bf16[8,9216,2304]{2,1,0:T(8,128)(2,1)} %param.21, bf16[6,96,2304]{2,1,0:T(8,128)(2,1)} %get-tuple-element.112, bf16[6,96,9216]{2,1,0:T(8,128)(2,1)} %multiply_convert_fusion.2.clone.3.clone.5), kind=kOutput, calls=%fused_computation.232 | convolution fusion | flops 24469143552 | bytes 58394880 | tf_op jit(solution)/shard_map/btf,fd->btd/dot_general | solution.py:52
  1189.8 21.4 %collective-permute-done.26 = bf16[6,48,4,256]{3,1,2,0:T(8,128)(2,1)S(1)} collective-permute-done((bf16[6,48,4,256]{3,1,2,0:T(8,128)(2,1)S(1)}, bf16[6,48,4,256]{3,1,2,0:T(8,128)(2,1)S(1)}, u32[]{:S(2)}, u32[]{:S(2)}) %collective-permute-start.26) | collective-permute-done | bytes 589856 | tf_op jit(solution)/shard_map/ppermute | solution.py:78
  1215.5 14.7 collective-permute-done.24
  1231.5 10.8 fusion.204
  1242.4 32.7 %fusion.18 = f32[6,96,9216]{2,1,0:T(8,128)} fusion(bf16[8,2304,9216]{2,1,0:T(8,128)(2,1)} %param.19, bf16[6,96,2304]{2,1,0:T(8,128)(2,1)} %get-tuple-element.118, f32[2304]{0:T(1024)S(1)} %copy-done.20, f32[6,96]{1,0:T(8,128)S(1)} %add_rsqrt_fusion.2), kind=kOutput, calls=%fused_computation.18 | convolution fusion | flops 24466489344 | bytes 66366720 | tf_op jit(solution)/shard_map/btd,df->btf/dot_general | solution.py:49
  1275.1 34.6 %multiply_convert_fusion.1.clone.3.clone.5 = bf16[6,96,9216]{2,1,0:T(8,128)(2,1)} fusion(f32[6,96,9216]{2,1,0:T(8,128)} %fusion.18, bf16[8,2304,9216]{2,1,0:T(8,128)(2,1)} %param.20, bf16[6,96,2304]{2,1,0:T(8,128)(2,1)} %get-tuple-element.118, f32[2304]{0:T(1024)S(1)} %copy-done.20, f32[6,96]{1,0:T(8,128)S(1)} %add_rsqrt_fusion.2), kind=kOutput, calls=%fused_computation.81.clone.clone.clone.clone.clone.clone.clone.2 | convolution fusion | flops 24498339840 | bytes 76983552 | tf_op jit(solution)/shard_map/btd,df->btf/dot_general | solution.py:50
  1309.6 33.9 %fusion.208 = (f32[6,96]{1,0:T(8,128)S(1)}, bf16[6,96,2304]{2,1,0:T(8,128)(2,1)S(1)}) fusion(bf16[8,9216,2304]{2,1,0:T(8,128)(2,1)} %param.21, bf16[6,96,2304]{2,1,0:T(8,128)(2,1)} %get-tuple-element.118, bf16[6,96,9216]{2,1,0:T(8,128)(2,1)} %multiply_convert_fusion.1.clone.3.clone.5), kind=kOutput, calls=%fused_computation.240 | convolution fusion | flops 24469143552 | bytes 58394880 | tf_op jit(solution)/shard_map/btf,fd->btd/dot_general | solution.py:52
  1368.6 21.4 %collective-permute-done.30 = bf16[6,48,4,256]{3,1,2,0:T(8,128)(2,1)S(1)} collective-permute-done((bf16[6,48,4,256]{3,1,2,0:T(8,128)(2,1)S(1)}, bf16[6,48,4,256]{3,1,2,0:T(8,128)(2,1)S(1)}, u32[]{:S(2)}, u32[]{:S(2)}) %collective-permute-start.30) | collective-permute-done | bytes 589856 | tf_op jit(solution)/shard_map/ppermute | solution.py:78
  1394.3 14.7 collective-permute-done.28
  1410.3 10.8 fusion.212
  1421.2 32.7 %fusion.12 = f32[6,96,9216]{2,1,0:T(8,128)} fusion(bf16[8,2304,9216]{2,1,0:T(8,128)(2,1)} %param.19, bf16[6,96,2304]{2,1,0:T(8,128)(2,1)} %get-tuple-element.124, f32[2304]{0:T(1024)S(1)} %copy-done.18, f32[6,96]{1,0:T(8,128)S(1)} %add_rsqrt_fusion), kind=kOutput, calls=%fused_computation.12 | convolution fusion | flops 24466489344 | bytes 66366720 | tf_op jit(solution)/shard_map/btd,df->btf/dot_general | solution.py:49
  1453.9 38.9 %multiply_convert_fusion.clone.7 = bf16[6,96,9216]{2,1,0:T(8,128)(2,1)} fusion(f32[6,96,9216]{2,1,0:T(8,128)} %fusion.12, bf16[8,2304,9216]{2,1,0:T(8,128)(2,1)} %param.20, bf16[6,96,2304]{2,1,0:T(8,128)(2,1)} %get-tuple-element.124, f32[2304]{0:T(1024)S(1)} %copy-done.18, f32[6,96]{1,0:T(8,128)S(1)} %add_rsqrt_fusion), kind=kOutput, calls=%fused_computation.80.clone.clone.clone.clone.clone.2 | convolution fusion | flops 24498339840 | bytes 76983552 | tf_op jit(solution)/shard_map/btd,df->btf/dot_general | solution.py:50
  1492.8 34.1 %fusion.215 = bf16[6,96,2304]{2,1,0:T(8,128)(2,1)} fusion(bf16[6,96,2304]{2,1,0:T(8,128)(2,1)S(1)} %copy-done.31, bf16[8,9216,2304]{2,1,0:T(8,128)(2,1)} %param.21, bf16[6,96,9216]{2,1,0:T(8,128)(2,1)} %multiply_convert_fusion.clone.7), kind=kOutput, calls=%fused_computation.247 | convolution fusion | flops 24465162240 | bytes 58392576 | tf_op jit(solution)/shard_map/btf,fd->btd/dot_general | solution.py:52
  (263 shorter events, 272.0 us)
Async XLA Ops:
  5.4 30.4 %copy-start.7 = (bf16[6,96,2304]{2,1,0:T(8,128)(2,1)S(1)}, bf16[6,96,2304]{2,1,0:T(8,128)(2,1)}, u32[]{:S(2)}) copy-start(bf16[6,96,2304]{2,1,0:T(8,128)(2,1)} %param.11) | copy-start | bytes 7962628
  39.1 111.6 %collective-permute-start.2 = (bf16[6,48,4,256]{3,1,2,0:T(8,128)(2,1)S(1)}, bf16[6,48,4,256]{3,1,2,0:T(8,128)(2,1)}, u32[]{:S(2)}, u32[]{:S(2)}) collective-permute-start(bf16[6,48,4,256]{3,1,2,0:T(8,128)(2,1)S(1)} %fusion.519), channel_id=1, source_target_pairs={{0,2},{1,3},{4,6},{5,7}} | collective-permute-start | bytes 1769480 | tf_op jit(solution)/shard_map/ppermute | solution.py:78
  44.1 106.6 %collective-permute-start.3 = (bf16[6,96,4,256]{3,1,2,0:T(8,128)(2,1)S(1)}, bf16[6,96,4,256]{3,1,2,0:T(8,128)(2,1)}, u32[]{:S(2)}, u32[]{:S(2)}) collective-permute-start(bf16[6,96,4,256]{3,1,2,0:T(8,128)(2,1)S(1)} %pad_maximum_fusion), channel_id=1, source_target_pairs={{0,1},{1,2},{2,3},{4,5},{5,6},{6,7}} | collective-permute-start | bytes 3538952 | tf_op jit(solution)/shard_map/ppermute | solution.py:77
  79.6 76.1 %collective-permute-start.1 = (bf16[6,96,4,256]{3,1,2,0:T(8,128)(2,1)}, bf16[6,96,4,256]{3,1,2,0:T(8,128)(2,1)}, u32[]{:S(2)}, u32[]{:S(2)}) collective-permute-start(bf16[6,96,4,256]{3,1,2,0:T(8,128)(2,1)} %fusion.504), channel_id=1, source_target_pairs={{0,1},{1,2},{2,3},{4,5},{5,6},{6,7}} | collective-permute-start | bytes 3538952 | tf_op jit(solution)/shard_map/ppermute | solution.py:77
  83.5 72.3 %collective-permute-start = (bf16[6,48,4,256]{3,1,2,0:T(8,128)(2,1)}, bf16[6,48,4,256]{3,1,2,0:T(8,128)(2,1)}, u32[]{:S(2)}, u32[]{:S(2)}) collective-permute-start(bf16[6,48,4,256]{3,1,2,0:T(8,128)(2,1)} %slice.480), channel_id=1, source_target_pairs={{0,2},{1,3},{4,6},{5,7}} | collective-permute-start | bytes 1769480 | tf_op jit(solution)/shard_map/ppermute | solution.py:78
  236.6 34.2 %copy-start.29 = (f32[2304]{0:T(1024)S(1)}, f32[2304]{0:T(1024)}, u32[]{:S(2)}) copy-start(f32[2304]{0:T(1024)} %get-tuple-element.18) | copy-start | bytes 27652
  282.9 34.0 %collective-permute-start.7 = (bf16[6,96,4,256]{3,1,2,0:T(8,128)(2,1)S(1)}, bf16[6,96,4,256]{3,1,2,0:T(8,128)(2,1)S(1)}, u32[]{:S(2)}, u32[]{:S(2)}) collective-permute-start(bf16[6,96,4,256]{3,1,2,0:T(8,128)(2,1)S(1)} %pad_maximum_fusion.1), channel_id=1, source_target_pairs={{0,1},{1,2},{2,3},{4,5},{5,6},{6,7}} | collective-permute-start | bytes 3538952 | tf_op jit(solution)/shard_map/ppermute | solution.py:77
  284.9 32.0 %collective-permute-start.6 = (bf16[6,48,4,256]{3,1,2,0:T(8,128)(2,1)S(1)}, bf16[6,48,4,256]{3,1,2,0:T(8,128)(2,1)S(1)}, u32[]{:S(2)}, u32[]{:S(2)}) collective-permute-start(bf16[6,48,4,256]{3,1,2,0:T(8,128)(2,1)S(1)} %fusion.518), channel_id=1, source_target_pairs={{0,2},{1,3},{4,6},{5,7}} | collective-permute-start | bytes 1769480 | tf_op jit(solution)/shard_map/ppermute | solution.py:78
  289.3 46.5 %collective-permute-start.5 = (bf16[6,96,4,256]{3,1,2,0:T(8,128)(2,1)S(1)}, bf16[6,96,4,256]{3,1,2,0:T(8,128)(2,1)S(1)}, u32[]{:S(2)}, u32[]{:S(2)}) collective-permute-start(bf16[6,96,4,256]{3,1,2,0:T(8,128)(2,1)S(1)} %fusion.505), channel_id=1, source_target_pairs={{0,1},{1,2},{2,3},{4,5},{5,6},{6,7}} | collective-permute-start | bytes 3538952 | tf_op jit(solution)/shard_map/ppermute | solution.py:77
  291.3 44.5 %collective-permute-start.4 = (bf16[6,48,4,256]{3,1,2,0:T(8,128)(2,1)S(1)}, bf16[6,48,4,256]{3,1,2,0:T(8,128)(2,1)S(1)}, u32[]{:S(2)}, u32[]{:S(2)}) collective-permute-start(bf16[6,48,4,256]{3,1,2,0:T(8,128)(2,1)S(1)} %slice.487), channel_id=1, source_target_pairs={{0,2},{1,3},{4,6},{5,7}} | collective-permute-start | bytes 1769480 | tf_op jit(solution)/shard_map/ppermute | solution.py:78
  337.1 10.9 copy-start.30
  415.3 34.1 %copy-start.27 = (f32[2304]{0:T(1024)S(1)}, f32[2304]{0:T(1024)}, u32[]{:S(2)}) copy-start(f32[2304]{0:T(1024)} %get-tuple-element.17) | copy-start | bytes 27652
  461.8 34.0 %collective-permute-start.11 = (bf16[6,96,4,256]{3,1,2,0:T(8,128)(2,1)S(1)}, bf16[6,96,4,256]{3,1,2,0:T(8,128)(2,1)S(1)}, u32[]{:S(2)}, u32[]{:S(2)}) collective-permute-start(bf16[6,96,4,256]{3,1,2,0:T(8,128)(2,1)S(1)} %pad_maximum_fusion.2), channel_id=1, source_target_pairs={{0,1},{1,2},{2,3},{4,5},{5,6},{6,7}} | collective-permute-start | bytes 3538952 | tf_op jit(solution)/shard_map/ppermute | solution.py:77
  463.8 32.0 %collective-permute-start.10 = (bf16[6,48,4,256]{3,1,2,0:T(8,128)(2,1)S(1)}, bf16[6,48,4,256]{3,1,2,0:T(8,128)(2,1)S(1)}, u32[]{:S(2)}, u32[]{:S(2)}) collective-permute-start(bf16[6,48,4,256]{3,1,2,0:T(8,128)(2,1)S(1)} %fusion.517), channel_id=1, source_target_pairs={{0,2},{1,3},{4,6},{5,7}} | collective-permute-start | bytes 1769480 | tf_op jit(solution)/shard_map/ppermute | solution.py:78
  470.0 44.7 %collective-permute-start.9 = (bf16[6,96,4,256]{3,1,2,0:T(8,128)(2,1)S(1)}, bf16[6,96,4,256]{3,1,2,0:T(8,128)(2,1)S(1)}, u32[]{:S(2)}, u32[]{:S(2)}) collective-permute-start(bf16[6,96,4,256]{3,1,2,0:T(8,128)(2,1)S(1)} %fusion.506), channel_id=1, source_target_pairs={{0,1},{1,2},{2,3},{4,5},{5,6},{6,7}} | collective-permute-start | bytes 3538952 | tf_op jit(solution)/shard_map/ppermute | solution.py:77
  472.3 42.4 %collective-permute-start.8 = (bf16[6,48,4,256]{3,1,2,0:T(8,128)(2,1)S(1)}, bf16[6,48,4,256]{3,1,2,0:T(8,128)(2,1)S(1)}, u32[]{:S(2)}, u32[]{:S(2)}) collective-permute-start(bf16[6,48,4,256]{3,1,2,0:T(8,128)(2,1)S(1)} %slice.494), channel_id=1, source_target_pairs={{0,2},{1,3},{4,6},{5,7}} | collective-permute-start | bytes 1769480 | tf_op jit(solution)/shard_map/ppermute | solution.py:78
  516.1 10.9 copy-start.28
  594.1 34.0 %copy-start.25 = (f32[2304]{0:T(1024)S(1)}, f32[2304]{0:T(1024)}, u32[]{:S(2)}) copy-start(f32[2304]{0:T(1024)} %get-tuple-element.16) | copy-start | bytes 27652
  640.6 34.0 %collective-permute-start.15 = (bf16[6,96,4,256]{3,1,2,0:T(8,128)(2,1)S(1)}, bf16[6,96,4,256]{3,1,2,0:T(8,128)(2,1)S(1)}, u32[]{:S(2)}, u32[]{:S(2)}) collective-permute-start(bf16[6,96,4,256]{3,1,2,0:T(8,128)(2,1)S(1)} %pad_maximum_fusion.3), channel_id=1, source_target_pairs={{0,1},{1,2},{2,3},{4,5},{5,6},{6,7}} | collective-permute-start | bytes 3538952 | tf_op jit(solution)/shard_map/ppermute | solution.py:77
  642.6 32.0 %collective-permute-start.14 = (bf16[6,48,4,256]{3,1,2,0:T(8,128)(2,1)S(1)}, bf16[6,48,4,256]{3,1,2,0:T(8,128)(2,1)S(1)}, u32[]{:S(2)}, u32[]{:S(2)}) collective-permute-start(bf16[6,48,4,256]{3,1,2,0:T(8,128)(2,1)S(1)} %fusion.516), channel_id=1, source_target_pairs={{0,2},{1,3},{4,6},{5,7}} | collective-permute-start | bytes 1769480 | tf_op jit(solution)/shard_map/ppermute | solution.py:78
  648.8 44.7 %collective-permute-start.13 = (bf16[6,96,4,256]{3,1,2,0:T(8,128)(2,1)S(1)}, bf16[6,96,4,256]{3,1,2,0:T(8,128)(2,1)S(1)}, u32[]{:S(2)}, u32[]{:S(2)}) collective-permute-start(bf16[6,96,4,256]{3,1,2,0:T(8,128)(2,1)S(1)} %fusion.507), channel_id=1, source_target_pairs={{0,1},{1,2},{2,3},{4,5},{5,6},{6,7}} | collective-permute-start | bytes 3538952 | tf_op jit(solution)/shard_map/ppermute | solution.py:77
  651.2 42.4 %collective-permute-start.12 = (bf16[6,48,4,256]{3,1,2,0:T(8,128)(2,1)S(1)}, bf16[6,48,4,256]{3,1,2,0:T(8,128)(2,1)S(1)}, u32[]{:S(2)}, u32[]{:S(2)}) collective-permute-start(bf16[6,48,4,256]{3,1,2,0:T(8,128)(2,1)S(1)} %slice.501), channel_id=1, source_target_pairs={{0,2},{1,3},{4,6},{5,7}} | collective-permute-start | bytes 1769480 | tf_op jit(solution)/shard_map/ppermute | solution.py:78
  694.9 10.9 copy-start.26
  773.2 34.0 %copy-start.23 = (f32[2304]{0:T(1024)S(1)}, f32[2304]{0:T(1024)}, u32[]{:S(2)}) copy-start(f32[2304]{0:T(1024)} %get-tuple-element.15) | copy-start | bytes 27652
  819.6 34.0 %collective-permute-start.19 = (bf16[6,96,4,256]{3,1,2,0:T(8,128)(2,1)S(1)}, bf16[6,96,4,256]{3,1,2,0:T(8,128)(2,1)S(1)}, u32[]{:S(2)}, u32[]{:S(2)}) collective-permute-start(bf16[6,96,4,256]{3,1,2,0:T(8,128)(2,1)S(1)} %pad_maximum_fusion.4), channel_id=1, source_target_pairs={{0,1},{1,2},{2,3},{4,5},{5,6},{6,7}} | collective-permute-start | bytes 3538952 | tf_op jit(solution)/shard_map/ppermute | solution.py:77
  821.6 32.0 %collective-permute-start.18 = (bf16[6,48,4,256]{3,1,2,0:T(8,128)(2,1)S(1)}, bf16[6,48,4,256]{3,1,2,0:T(8,128)(2,1)S(1)}, u32[]{:S(2)}, u32[]{:S(2)}) collective-permute-start(bf16[6,48,4,256]{3,1,2,0:T(8,128)(2,1)S(1)} %fusion.515), channel_id=1, source_target_pairs={{0,2},{1,3},{4,6},{5,7}} | collective-permute-start | bytes 1769480 | tf_op jit(solution)/shard_map/ppermute | solution.py:78
  827.8 44.7 %collective-permute-start.17 = (bf16[6,96,4,256]{3,1,2,0:T(8,128)(2,1)S(1)}, bf16[6,96,4,256]{3,1,2,0:T(8,128)(2,1)S(1)}, u32[]{:S(2)}, u32[]{:S(2)}) collective-permute-start(bf16[6,96,4,256]{3,1,2,0:T(8,128)(2,1)S(1)} %fusion.508), channel_id=1, source_target_pairs={{0,1},{1,2},{2,3},{4,5},{5,6},{6,7}} | collective-permute-start | bytes 3538952 | tf_op jit(solution)/shard_map/ppermute | solution.py:77
  830.2 42.4 %collective-permute-start.16 = (bf16[6,48,4,256]{3,1,2,0:T(8,128)(2,1)S(1)}, bf16[6,48,4,256]{3,1,2,0:T(8,128)(2,1)S(1)}, u32[]{:S(2)}, u32[]{:S(2)}) collective-permute-start(bf16[6,48,4,256]{3,1,2,0:T(8,128)(2,1)S(1)} %slice.508), channel_id=1, source_target_pairs={{0,2},{1,3},{4,6},{5,7}} | collective-permute-start | bytes 1769480 | tf_op jit(solution)/shard_map/ppermute | solution.py:78
  873.9 10.9 copy-start.24
  952.0 34.0 %copy-start.21 = (f32[2304]{0:T(1024)S(1)}, f32[2304]{0:T(1024)}, u32[]{:S(2)}) copy-start(f32[2304]{0:T(1024)} %get-tuple-element.14) | copy-start | bytes 27652
  998.5 34.0 %collective-permute-start.23 = (bf16[6,96,4,256]{3,1,2,0:T(8,128)(2,1)S(1)}, bf16[6,96,4,256]{3,1,2,0:T(8,128)(2,1)S(1)}, u32[]{:S(2)}, u32[]{:S(2)}) collective-permute-start(bf16[6,96,4,256]{3,1,2,0:T(8,128)(2,1)S(1)} %pad_maximum_fusion.5), channel_id=1, source_target_pairs={{0,1},{1,2},{2,3},{4,5},{5,6},{6,7}} | collective-permute-start | bytes 3538952 | tf_op jit(solution)/shard_map/ppermute | solution.py:77
  1000.5 32.0 %collective-permute-start.22 = (bf16[6,48,4,256]{3,1,2,0:T(8,128)(2,1)S(1)}, bf16[6,48,4,256]{3,1,2,0:T(8,128)(2,1)S(1)}, u32[]{:S(2)}, u32[]{:S(2)}) collective-permute-start(bf16[6,48,4,256]{3,1,2,0:T(8,128)(2,1)S(1)} %fusion.514), channel_id=1, source_target_pairs={{0,2},{1,3},{4,6},{5,7}} | collective-permute-start | bytes 1769480 | tf_op jit(solution)/shard_map/ppermute | solution.py:78
  1006.7 44.7 %collective-permute-start.21 = (bf16[6,96,4,256]{3,1,2,0:T(8,128)(2,1)S(1)}, bf16[6,96,4,256]{3,1,2,0:T(8,128)(2,1)S(1)}, u32[]{:S(2)}, u32[]{:S(2)}) collective-permute-start(bf16[6,96,4,256]{3,1,2,0:T(8,128)(2,1)S(1)} %fusion.509), channel_id=1, source_target_pairs={{0,1},{1,2},{2,3},{4,5},{5,6},{6,7}} | collective-permute-start | bytes 3538952 | tf_op jit(solution)/shard_map/ppermute | solution.py:77
  1009.0 42.4 %collective-permute-start.20 = (bf16[6,48,4,256]{3,1,2,0:T(8,128)(2,1)S(1)}, bf16[6,48,4,256]{3,1,2,0:T(8,128)(2,1)S(1)}, u32[]{:S(2)}, u32[]{:S(2)}) collective-permute-start(bf16[6,48,4,256]{3,1,2,0:T(8,128)(2,1)S(1)} %slice.515), channel_id=1, source_target_pairs={{0,2},{1,3},{4,6},{5,7}} | collective-permute-start | bytes 1769480 | tf_op jit(solution)/shard_map/ppermute | solution.py:78
  1052.8 10.9 copy-start.22
  1130.7 34.1 %copy-start.19 = (f32[2304]{0:T(1024)S(1)}, f32[2304]{0:T(1024)}, u32[]{:S(2)}) copy-start(f32[2304]{0:T(1024)} %get-tuple-element.20) | copy-start | bytes 27652
  1177.2 34.0 %collective-permute-start.27 = (bf16[6,96,4,256]{3,1,2,0:T(8,128)(2,1)S(1)}, bf16[6,96,4,256]{3,1,2,0:T(8,128)(2,1)S(1)}, u32[]{:S(2)}, u32[]{:S(2)}) collective-permute-start(bf16[6,96,4,256]{3,1,2,0:T(8,128)(2,1)S(1)} %pad_maximum_fusion.6), channel_id=1, source_target_pairs={{0,1},{1,2},{2,3},{4,5},{5,6},{6,7}} | collective-permute-start | bytes 3538952 | tf_op jit(solution)/shard_map/ppermute | solution.py:77
  1179.2 32.0 %collective-permute-start.26 = (bf16[6,48,4,256]{3,1,2,0:T(8,128)(2,1)S(1)}, bf16[6,48,4,256]{3,1,2,0:T(8,128)(2,1)S(1)}, u32[]{:S(2)}, u32[]{:S(2)}) collective-permute-start(bf16[6,48,4,256]{3,1,2,0:T(8,128)(2,1)S(1)} %fusion.513), channel_id=1, source_target_pairs={{0,2},{1,3},{4,6},{5,7}} | collective-permute-start | bytes 1769480 | tf_op jit(solution)/shard_map/ppermute | solution.py:78
  1185.5 44.7 %collective-permute-start.25 = (bf16[6,96,4,256]{3,1,2,0:T(8,128)(2,1)S(1)}, bf16[6,96,4,256]{3,1,2,0:T(8,128)(2,1)S(1)}, u32[]{:S(2)}, u32[]{:S(2)}) collective-permute-start(bf16[6,96,4,256]{3,1,2,0:T(8,128)(2,1)S(1)} %fusion.510), channel_id=1, source_target_pairs={{0,1},{1,2},{2,3},{4,5},{5,6},{6,7}} | collective-permute-start | bytes 3538952 | tf_op jit(solution)/shard_map/ppermute | solution.py:77
  1187.8 42.4 %collective-permute-start.24 = (bf16[6,48,4,256]{3,1,2,0:T(8,128)(2,1)S(1)}, bf16[6,48,4,256]{3,1,2,0:T(8,128)(2,1)S(1)}, u32[]{:S(2)}, u32[]{:S(2)}) collective-permute-start(bf16[6,48,4,256]{3,1,2,0:T(8,128)(2,1)S(1)} %slice.522), channel_id=1, source_target_pairs={{0,2},{1,3},{4,6},{5,7}} | collective-permute-start | bytes 1769480 | tf_op jit(solution)/shard_map/ppermute | solution.py:78
  1231.5 10.9 copy-start.20
  1309.6 33.9 %copy-start.17 = (f32[2304]{0:T(1024)S(1)}, f32[2304]{0:T(1024)}, u32[]{:S(2)}) copy-start(f32[2304]{0:T(1024)} %get-tuple-element.13) | copy-start | bytes 27652
  1356.0 34.0 %collective-permute-start.31 = (bf16[6,96,4,256]{3,1,2,0:T(8,128)(2,1)S(1)}, bf16[6,96,4,256]{3,1,2,0:T(8,128)(2,1)S(1)}, u32[]{:S(2)}, u32[]{:S(2)}) collective-permute-start(bf16[6,96,4,256]{3,1,2,0:T(8,128)(2,1)S(1)} %pad_maximum_fusion.7), channel_id=1, source_target_pairs={{0,1},{1,2},{2,3},{4,5},{5,6},{6,7}} | collective-permute-start | bytes 3538952 | tf_op jit(solution)/shard_map/ppermute | solution.py:77
  1358.0 32.0 %collective-permute-start.30 = (bf16[6,48,4,256]{3,1,2,0:T(8,128)(2,1)S(1)}, bf16[6,48,4,256]{3,1,2,0:T(8,128)(2,1)S(1)}, u32[]{:S(2)}, u32[]{:S(2)}) collective-permute-start(bf16[6,48,4,256]{3,1,2,0:T(8,128)(2,1)S(1)} %fusion.512), channel_id=1, source_target_pairs={{0,2},{1,3},{4,6},{5,7}} | collective-permute-start | bytes 1769480 | tf_op jit(solution)/shard_map/ppermute | solution.py:78
  1364.2 44.7 %collective-permute-start.29 = (bf16[6,96,4,256]{3,1,2,0:T(8,128)(2,1)S(1)}, bf16[6,96,4,256]{3,1,2,0:T(8,128)(2,1)S(1)}, u32[]{:S(2)}, u32[]{:S(2)}) collective-permute-start(bf16[6,96,4,256]{3,1,2,0:T(8,128)(2,1)S(1)} %fusion.511), channel_id=1, source_target_pairs={{0,1},{1,2},{2,3},{4,5},{5,6},{6,7}} | collective-permute-start | bytes 3538952 | tf_op jit(solution)/shard_map/ppermute | solution.py:77
  1366.6 42.4 %collective-permute-start.28 = (bf16[6,48,4,256]{3,1,2,0:T(8,128)(2,1)S(1)}, bf16[6,48,4,256]{3,1,2,0:T(8,128)(2,1)S(1)}, u32[]{:S(2)}, u32[]{:S(2)}) collective-permute-start(bf16[6,48,4,256]{3,1,2,0:T(8,128)(2,1)S(1)} %slice.529), channel_id=1, source_target_pairs={{0,2},{1,3},{4,6},{5,7}} | collective-permute-start | bytes 1769480 | tf_op jit(solution)/shard_map/ppermute | solution.py:78
  1410.3 10.9 copy-start.18
  1453.9 39.0 %copy-start.31 = (bf16[6,96,2304]{2,1,0:T(8,128)(2,1)S(1)}, bf16[6,96,2304]{2,1,0:T(8,128)(2,1)}, u32[]{:S(2)}) copy-start(bf16[6,96,2304]{2,1,0:T(8,128)(2,1)} %get-tuple-element.124) | copy-start | bytes 7962628
  (30 other events, 198.4 us)
where the time goes:
time: 1530 us
  matrix products  1050 us (69%)
  waiting for transfers between devices  255 us (17%)
  local copies, waits for them, and re-layouts  114 us (7%)
  starting transfers between devices  70.6 us (5%)
  other arithmetic  36.1 us (2%)
    dot_general x8, matrix products, mlp_block(): jnp.einsum('btd,df->btf', normed, up_weight, preferred_element_type=jnp.f...  280 us
    dot_general x8, matrix products, mlp_block(): jnp.einsum('btf,fd->btd', activated, down_weight, preferred_element_type=...  272 us
    dot_general x8, matrix products, mlp_block(): jnp.einsum('btd,df->btf', normed, gate_weight, preferred_element_type=jnp...  262 us
    ppermute x16, waiting for transfers between devices, local_stack(): lax.ppermute((keys[:, seq_dev - tail_len:], values[:, seq_dev - tail_len:...  255 us
    dot_general x8, matrix products, local_stack(): jnp.einsum('bthe,hed->btd', attn_vals, w_out[layer], preferred_element_ty...  86.7 us
    dot_general x8, matrix products, project_qkv(): jnp.einsum('btd,dhe->bthe', normed, q_weight, preferred_element_type=jnp....  72.8 us
    slice x1, local copies, waits for them, and re-layouts, local_stack(): w_query[layer]  49.1 us
    ppermute x16, starting transfers between devices, local_stack(): lax.ppermute((keys[:, seq_dev - tail_len:], values[:, seq_dev - tail_len:...  37.2 us
  transfers between devices with their start and end apart: 32, of which 14 were waited for; matrix products, arithmetic and copies ran while one was open for 11% of the time, Pallas kernels for 0%

commit v1 on v0

v1 whole, which is shorter than its diff:
```python
import functools

import jax
import jax.numpy as jnp
from jax import lax
from jax.experimental import pallas as pl
from jax.experimental.pallas import tpu as pltpu
from jax.sharding import PartitionSpec as P

EPSILON = 1e-5
THETA = 10000.0
LAYERS, D, HEADS, KV, HD, FF = 8, 2304, 8, 4, 256, 9216
SEQ, HALF = 384, 192
ROWS = SEQ + HALF
WINDOW = 144
PAD = 160
QB = 96
CTX = PAD + QB
WHOLE_KEYS = PAD + SEQ
KEYS = WHOLE_KEYS + PAD + HALF
FC = 512
NF = FF // FC
GW = 256
KC = 1024
NO, ND = HEADS * HD // KC, FF // KC
SLAB = 128
NS = D // SLAB
NB = 192
NW = D // 3
WREL = 2 * KV * HD + HEADS * HD
MESH = pl.DeviceIdType.MESH
F32, BF16 = jnp.float32, jnp.bfloat16


def dot(a, b):
    return jnp.dot(a, b, preferred_element_type=F32)


def rope_tables(positions):
    half = HD // 2
    inv_freq = THETA ** (-(jnp.arange(half, dtype=F32) * 2.0) / HD)
    angles = positions.astype(F32)[:, None] * inv_freq
    return jnp.cos(angles), jnp.sin(angles)


def stack_kernel(x_hbm, cos_ref, sin_ref, ga_ref, gm_ref, wq, wk, wv, wo, wg, wu, wd, out_hbm,
                 x, h, wrel, q, k, v, acc, bias, rq, rk, rv, gb, ub, db,
                 sx, sq, sk, sv, sg, su, sd, send_sem, recv_sem, credit):
    me = lax.axis_index('sp')
    core = lax.rem(me, 2)
    partner = {'sp': me + 1 - 2 * core}

    def slab_copies(l, i):
        s = lax.rem(l * NS + i, 2)
        rows = pl.ds(i * SLAB, SLAB)
        return (pltpu.make_async_copy(wq.at[l, rows], rq.at[s], sq.at[s]),
                pltpu.make_async_copy(wk.at[l, rows], rk.at[s], sk.at[s]),
                pltpu.make_async_copy(wv.at[l, rows], rv.at[s], sv.at[s]))

    def gate_copies(l, i):
        s = lax.rem(i, 2)
        cols = pl.ds(i * FC, FC)
        return (pltpu.make_async_copy(wg.at[l, :, cols], gb.at[s], sg.at[s]),
                pltpu.make_async_copy(wu.at[l, :, cols], ub.at[s], su.at[s]))

    def out_copies(l, i):
        s = lax.rem(l * (NO + ND) + i, 2)
        return (pltpu.make_async_copy(wo.at[l, pl.ds(i * KC, KC)], db.at[s], sd.at[s]),)

    def down_copies(l, i):
        s = lax.rem(l * (NO + ND) + NO + i, 2)
        return (pltpu.make_async_copy(wd.at[l, pl.ds(i * KC, KC)], db.at[s], sd.at[s]),)

    def start(copies):
        for c in copies:
            c.start()

    def wait(copies):
        for c in copies:
            c.wait()

    def rms_norm(gain_ref, l):
        gain = gain_ref[pl.ds(l, 1), :]

        def block(b, _):
            rows = pl.ds(pl.multiple_of(b * NB, NB), NB)
            xf = x[rows].astype(F32)
            inv = lax.rsqrt(jnp.mean(xf * xf, axis=-1, keepdims=True) + EPSILON)
            h[rows] = (xf * inv * gain).astype(BF16)
            return 0

        lax.fori_loop(0, ROWS // NB, block, 0)

    def rotated(t):
        cos_t, sin_t = cos_ref[...], sin_ref[...]
        a, b = t[:, :HD // 2], t[:, HD // 2:]
        return jnp.concatenate([a * cos_t - b * sin_t, b * cos_t + a * sin_t], axis=-1).astype(BF16)

    def store_keys(ref, head, t):
        ref[head, PAD:WHOLE_KEYS] = t[:SEQ]
        ref[head, WHOLE_KEYS + PAD:KEYS] = t[SEQ:]

    def halo_copies():
        src, dst = pl.ds(KEYS - PAD, PAD), pl.ds(WHOLE_KEYS, PAD)
        return [pltpu.make_async_remote_copy(
            src_ref=ref.at[:, src], dst_ref=ref.at[:, dst], send_sem=send_sem.at[n], recv_sem=recv_sem.at[n],
            device_id=partner, device_id_type=MESH) for n, ref in enumerate((k, v))]

    def attend(q_row, key_row, variant):
        mask = bias[variant]
        for g in range(KV):
            qs = jnp.concatenate([q[2 * g, pl.ds(q_row, QB)], q[2 * g + 1, pl.ds(q_row, QB)]], axis=0)
            kc, vc = k[g, pl.ds(key_row, CTX)], v[g, pl.ds(key_row, CTX)]
            s = lax.dot_general(qs, kc, (((1,), (1,)), ((), ())), preferred_element_type=F32)
            s = s * HD ** -0.5 + jnp.concatenate([mask, mask], axis=0)
            e = jnp.exp(s - jnp.max(s, axis=-1, keepdims=True))
            p = (e * (1.0 / jnp.sum(e, axis=-1, keepdims=True))).astype(BF16)
            o = dot(p, vc).astype(BF16)
            q[2 * g, pl.ds(q_row, QB)] = o[:QB]
            q[2 * g + 1, pl.ds(q_row, QB)] = o[QB:]

    barrier = pltpu.get_barrier_semaphore()
    pl.semaphore_signal(barrier, inc=1, device_id=partner, device_id_type=MESH)
    pl.semaphore_wait(barrier, 1)

    x_in = pltpu.make_async_copy(x_hbm, x, sx)
    x_in.start()
    start(slab_copies(0, 0))
    start(slab_copies(0, 1))
    start(out_copies(0, 0))
    start(out_copies(0, 1))
    start(gate_copies(0, 0))
    start(gate_copies(0, 1))

    k[:, 0:PAD] = jnp.zeros((KV, PAD, HD), BF16)
    v[:, 0:PAD] = jnp.zeros((KV, PAD, HD), BF16)
    row = lax.broadcasted_iota(jnp.int32, (QB, CTX), 0)
    col = lax.broadcasted_iota(jnp.int32, (QB, CTX), 1)
    distance = row + PAD - col
    band = (distance >= 0) & (distance < WINDOW)
    for n, first in enumerate((PAD, PAD - QB, 0)):
        bias[n] = jnp.where(band & (col >= first), 0.0, -jnp.inf).astype(F32)
    x_in.wait()

    def layer(l, _):
        rms_norm(ga_ref, l)

        def relayout(i, _):
            s = lax.rem(l * NS + i, 2)
            wait(slab_copies(l, i))
            rows = pl.ds(pl.multiple_of(i * SLAB, SLAB), SLAB)
            wrel[rows, 0:KV * HD] = pltpu.einshape("dhe->d(he)", rk[s])
            wrel[rows, KV * HD:2 * KV * HD] = pltpu.einshape("dhe->d(he)", rv[s])
            wrel[rows, 2 * KV * HD:] = pltpu.einshape("dhe->d(he)", rq[s])

            @pl.when(i + 2 < NS)
            def _():
                start(slab_copies(l, i + 2))

            @pl.when((i + 2 >= NS) & (l + 1 < LAYERS))
            def _():
                start(slab_copies(l + 1, i + 2 - NS))
            return 0

        lax.fori_loop(0, NS, relayout, 0)

        def key_step(i, _):
            t = dot(h[...], wrel[:, pl.ds(pl.multiple_of(i * 2 * HD, 2 * HD), 2 * HD)])
            for j in range(2):
                store_keys(k, 2 * i + j, rotated(t[:, j * HD:(j + 1) * HD]))
            return 0

        def value_step(i, _):
            t = dot(h[...], wrel[:, pl.ds(pl.multiple_of((KV + 2 * i) * HD, 2 * HD), 2 * HD)])
            for j in range(2):
                store_keys(v, 2 * i + j, t[:, j * HD:(j + 1) * HD].astype(BF16))
            return 0

        def query_step(i, _):
            t = dot(h[...], wrel[:, pl.ds(pl.multiple_of((2 * KV + 2 * i) * HD, 2 * HD), 2 * HD)])
            for j in range(2):
                q[2 * i + j] = rotated(t[:, j * HD:(j + 1) * HD])
            return 0

        lax.fori_loop(0, KV // 2, key_step, 0)
        lax.fori_loop(0, KV // 2, value_step, 0)

        @pl.when(l > 0)
        def _():
            pl.semaphore_wait(credit, 1)

        halo = halo_copies()
        start(halo)
        lax.fori_loop(0, HEADS // 2, query_step, 0)

        def whole_step(b, _):
            r = pl.multiple_of(b * QB, QB)
            attend(r, r, jnp.minimum(b, 2))
            return 0

        def half_step(b, _):
            r = pl.multiple_of(b * QB, QB)
            attend(SEQ + r, WHOLE_KEYS + r, b + (2 - b) * core)
            return 0

        lax.fori_loop(0, SEQ // QB, whole_step, 0)
        wait(halo)
        lax.fori_loop(0, HALF // QB, half_step, 0)

        @pl.when(l + 1 < LAYERS)
        def _():
            pl.semaphore_signal(credit, inc=1, device_id=partner, device_id_type=MESH)

        acc[...] = x[...].astype(F32)

        def out_step(i, _):
            wait(out_copies(l, i))
            s = lax.rem(l * (NO + ND) + i, 2)
            heads = KC // HD
            o = jnp.concatenate([q[heads * i + j] for j in range(heads)], axis=1)
            for n in range(0, D, NW):
                acc[:, n:n + NW] += dot(o, db[s, :, n:n + NW])
            start(down_copies(l, i))
            return 0

        lax.fori_loop(0, NO, out_step, 0)
        x[...] = acc[...].astype(BF16)
        rms_norm(gm_ref, l)

        def gate_step(i, _):
            wait(gate_copies(l, i))
            s = lax.rem(i, 2)
            per = WREL // FC
            rows = pl.ds(pl.multiple_of((i // per) * ROWS, ROWS), ROWS)
            first = lax.rem(i, per) * FC
            for n in range(0, FC, GW):
                g = dot(h[...], gb[s, :, n:n + GW])
                u = dot(h[...], ub[s, :, n:n + GW])
                wrel[rows, pl.ds(pl.multiple_of(first + n, GW), GW)] = (g * (1.0 / (1.0 + jnp.exp(-g))) * u).astype(BF16)

            @pl.when(i + 2 < NF)
            def _():
                start(gate_copies(l, i + 2))

            @pl.when((i + 2 >= NF) & (l + 1 < LAYERS))
            def _():
                start(gate_copies(l + 1, i + 2 - NF))
            return 0

        lax.fori_loop(0, NF, gate_step, 0)
        acc[...] = x[...].astype(F32)

        def down_step(i, _):
            wait(down_copies(l, i))
            s = lax.rem(l * (NO + ND) + NO + i, 2)
            per = WREL // KC
            rows = pl.ds(pl.multiple_of((i // per) * ROWS, ROWS), ROWS)
            cols = pl.ds(pl.multiple_of(lax.rem(i, per) * KC, KC), KC)
            for n in range(0, D, NW):
                acc[:, n:n + NW] += dot(wrel[rows, cols], db[s, :, n:n + NW])

            @pl.when(i + 2 < ND)
            def _():
                start(down_copies(l, i + 2))

            @pl.when((i + 2 >= ND) & (l + 1 < LAYERS))
            def _():
                start(out_copies(l + 1, i + 2 - ND))
            return 0

        lax.fori_loop(0, ND, down_step, 0)
        x[...] = acc[...].astype(BF16)
        return 0

    lax.fori_loop(0, LAYERS, layer, 0)
    x_out = pltpu.make_async_copy(x, out_hbm, sx)
    x_out.start()
    x_out.wait()


def run_stack(x, cos_t, sin_t, *weights):
    vmem, hbm = pl.BlockSpec(memory_space=pltpu.VMEM), pl.BlockSpec(memory_space=pltpu.HBM)
    dma = pltpu.SemaphoreType.DMA
    return pl.pallas_call(
        stack_kernel,
        out_shape=jax.ShapeDtypeStruct((ROWS, D), BF16),
        in_specs=[hbm] + [vmem] * 4 + [hbm] * 7,
        out_specs=hbm,
        scratch_shapes=[
            pltpu.VMEM((ROWS, D), BF16),
            pltpu.VMEM((ROWS, D), BF16),
            pltpu.VMEM((D, WREL), BF16),
            pltpu.VMEM((HEADS, ROWS, HD), BF16),
            pltpu.VMEM((KV, KEYS, HD), BF16),
            pltpu.VMEM((KV, KEYS, HD), BF16),
            pltpu.VMEM((ROWS, D), F32),
            pltpu.VMEM((3, QB, CTX), F32),
            pltpu.VMEM((2, SLAB, HEADS, HD), BF16),
            pltpu.VMEM((2, SLAB, KV, HD), BF16),
            pltpu.VMEM((2, SLAB, KV, HD), BF16),
            pltpu.VMEM((2, D, FC), BF16),
            pltpu.VMEM((2, D, FC), BF16),
            pltpu.VMEM((2, KC, D), BF16),
            dma, dma((2,)), dma((2,)), dma((2,)), dma((2,)), dma((2,)), dma((2,)),
            dma((2,)), dma((2,)), pltpu.SemaphoreType.REGULAR,
        ],
        compiler_params=pltpu.CompilerParams(
            vmem_limit_bytes=67043328, collective_id=0, has_side_effects=True),
        name='decoder_stack',
    )(x, cos_t, sin_t, *weights)


def half_perm(r):
    return [(2 * x + c, 2 * (c ^ r) + x) for x in range(2) for c in range(2)]


def to_sequences(blocks, core):
    whole = lax.all_to_all(jnp.stack([blocks[0], blocks[2], blocks[3], blocks[5]]), 'sp', 0, 0)
    flip = lax.axis_index('sp') >= 2
    first = lax.ppermute(jnp.where(core == 0, blocks[1], blocks[4]), 'sp', half_perm(0))
    second = lax.ppermute(jnp.where(core == 0, blocks[4], blocks[1]), 'sp', half_perm(1))
    low, high = jnp.where(flip, second, first), jnp.where(flip, first, second)
    return jnp.concatenate([whole.reshape(SEQ, -1), low, high], axis=0)


def to_shards(rows, core):
    blocks = rows.reshape(ROWS // QB, QB, -1)
    whole = lax.all_to_all(blocks[:4], 'sp', 0, 0)
    flip = lax.axis_index('sp') >= 2
    inverse = [[(b, a) for a, b in half_perm(r)] for r in range(2)]
    first = lax.ppermute(jnp.where(flip, blocks[5], blocks[4]), 'sp', inverse[0])
    second = lax.ppermute(jnp.where(flip, blocks[4], blocks[5]), 'sp', inverse[1])
    one, four = jnp.where(core == 0, first, second), jnp.where(core == 0, second, first)
    return jnp.stack([whole[0], one, whole[1], whole[2], four, whole[3]])


def solution(mesh):
    def local_stack(hidden_states, positions, gain_attn, gain_mlp, w_query, w_key, w_value, w_out, w_gate, w_up, w_down):
        core = lax.rem(lax.axis_index('sp'), 2)
        every = lax.all_gather(positions, 'sp', axis=1, tiled=True)
        chip = lax.axis_index('sp') // 2
        whole_pos = lax.dynamic_slice_in_dim(every, 3 * chip + 2 * core, 1, axis=0)[0]
        half_pos = lax.dynamic_slice(every, (3 * chip + 1, HALF * core), (1, HALF))[0]
        cos_t, sin_t = rope_tables(jnp.concatenate([whole_pos, half_pos]))
        x = to_sequences(hidden_states, core)
        out = run_stack(x, cos_t, sin_t, gain_attn, gain_mlp, w_query, w_key, w_value,
                        w_out.reshape(LAYERS, HEADS * HD, D), w_gate, w_up, w_down)
        return to_shards(out, core)

    row_spec = P('dp', 'sp', None)
    return jax.shard_map(local_stack, mesh=mesh, in_specs=(row_spec, P('dp', 'sp'), P(), P(), P(), P(), P(), P(), P(), P(), P()), out_specs=row_spec, check_vma=False)
```

time: 1530 us -> 1060 us (0.69)
  matrix products: 1050 us -> 0 us
  Pallas kernels: 0 us -> 969 us
  waiting for transfers between devices: 255 us -> 25.9 us
  local copies, waits for them, and re-layouts: 114 us -> 7.44 us
  starting transfers between devices: 70.6 us -> 15.4 us
  blocking collectives: 0 us -> 28.4 us
  other arithmetic: 36.1 us -> 8.13 us
    dot_general x72 -> x0, matrix products: 1050 us -> none  [the longest x8 280 us: mlp_block(): jnp.einsum('btd,df->btf', normed, up_weight, preferred_element_type=jnp.f...]
    pallas_call x0 -> x1, Pallas kernels: none -> 969 us  [run_stack(): pl.pallas_call(stack_kernel, out_shape=jax.ShapeDtypeStruct((ROWS, D), BF...]
    ppermute x32 -> x4, waiting for transfers between devices: 255 us -> 9.72 us  [the longest x1 6.56 us: to_shards(): lax.ppermute(jnp.where(flip, blocks[5], blocks[4]), 'sp', inverse[0])]
    slice x13 -> x3, local copies, waits for them, and re-layouts: 114 us -> 2.88 us  [the longest x1 2.8 us: to_shards(): whole = lax.all_to_all(blocks[:4], 'sp', 0, 0)]
    ppermute x32 -> x4, starting transfers between devices: 70.6 us -> 7.42 us  [the longest x1 3.85 us: to_sequences(): lax.ppermute(jnp.where(core == 0, blocks[1], blocks[4]), 'sp', half_perm(0))]
    all_gather x0 -> x1, blocking collectives: none -> 28.4 us  [local_stack(): every = lax.all_gather(positions, 'sp', axis=1, tiled=True)]
    sub x8 -> x0, other arithmetic: 19.7 us -> none  [attend(): attn_probs = jax.nn.softmax(scores, axis=-1).astype(jnp.bfloat16)]
    all_to_all x0 -> x2, waiting for transfers between devices: none -> 16.2 us  [the longest x1 16.2 us: to_shards(): whole = lax.all_to_all(blocks[:4], 'sp', 0, 0)]
  transfers between devices with their start and end apart: 32 -> 6, of which waited for: 14 -> 3; matrix products, arithmetic and copies ran while one was open for 11% -> 1% of each run, Pallas kernels for 0% -> 0%
where the time goes in v1:
time: 1060 us; the launch traced here: 1050 us
  Pallas kernels  969 us (91%)
  blocking collectives  28.4 us (3%)
  waiting for transfers between devices  25.9 us (2%)
  starting transfers between devices  15.4 us (1%)
    pallas_call x1, Pallas kernels, run_stack(): pl.pallas_call(stack_kernel, out_shape=jax.ShapeDtypeStruct((ROWS, D), BF...  969 us
    all_gather x1, blocking collectives, local_stack(): every = lax.all_gather(positions, 'sp', axis=1, tiled=True)  28.4 us
  transfers between devices with their start and end apart: 6, of which 3 were waited for; matrix products, arithmetic and copies ran while one was open for 1% of the time, Pallas kernels for 0%

profile of v1, /device:TPU:1, one launch (start us, length us, event | category | flops | bytes accessed | tf_op | source)
XLA Modules:
  0.0 1054.6 jit_solution(4650031526020763092)
XLA Ops:
  0.0 0.0 slice-start
  0.0 1.6 fusion
  1.6 0.1 slice-done
  1.7 1.4 pad_maximum_fusion.1
  3.1 0.0 copy-start.1
  3.1 4.4 all-to-all-start
  7.5 0.0 collective-permute-start
  7.5 3.9 collective-permute-start.1
  11.4 0.0 copy-done.1
  11.4 28.4 %all-gather = s32[4,96,6]{1,2,0:T(8,128)S(1)} all-gather(s32[1,96,6]{1,2,0:T(8,128)S(1)} %bitcast.18), channel_id=1, replica_groups=mesh['dp'=2,'sp'=4] {'sp'}, dimensions={0}, use_global_device_ids=true | all-gather | bytes 11520 | tf_op jit(solution)/shard_map/all_gather | solution.py:340
  39.8 0.7 reshape.43
  40.5 0.8 dynamic-slice.1
  41.3 0.7 dynamic-slice_reduce_fusion
  42.0 1.9 multiply_sine_fusion
  44.0 0.0 collective-permute-done
  44.0 0.0 collective-permute-done.1
  44.0 0.1 broadcast_select_fusion.3
  44.1 0.0 all-to-all-done
  44.1 1.7 pad_maximum_fusion.x_hbm
  45.7 969.1 %decoder_stack.1 = bf16[576,2304]{1,0:T(8,128)(2,1)} custom-call(bf16[576,2304]{1,0:T(8,128)(2,1)} %pad_maximum_fusion.x_hbm, f32[576,128]{1,0:T(8,128)} %get-tuple-element.14.cos_ref, f32[576,128]{1,0:T(8,128)} %get-tuple-element.13.sin_ref, f32[8,2304]{1,0:T(8,128)} %ga_ref.1, f32[8,2304]{1,0:T(8,128)} %gm_ref.1, bf16[8,2304,8,256]{3,2,1,0:T(8,128)(2,1)} %wq.1, ...), custom_call_target="tpu_custom_call" | custom-call | tf_op jit(solution)/shard_map/decoder_stack/pallas_call | solution.py:284
  1014.9 2.8 slice.51
  1017.7 3.6 all-to-all-start.1
  1021.3 1.2 broadcast_select_fusion
  1022.5 1.4 collective-permute-start.3
  1023.9 2.2 collective-permute-start.2
  1026.0 16.2 %all-to-all-done.1 = bf16[4,96,2304]{2,1,0:T(8,128)(2,1)S(1)} async-done(((bf16[4,96,2304]{2,1,0:T(8,128)(2,1)}), bf16[4,96,2304]{2,1,0:T(8,128)(2,1)S(1)}, u32[]{:S(2)}, u32[]{:S(2)}) %all-to-all-start.1) | async-done | bytes 1769504 | tf_op jit(solution)/shard_map/all_to_all | solution.py:328
  1042.3 3.2 collective-permute-done.3
  1045.4 6.6 collective-permute-done.2
  1052.0 0.1 bitcast_dynamic-update-slice_fusion.1
  1052.1 0.1 slice_dynamic-update-slice_fusion
  1052.2 0.1 bitcast_dynamic-update-slice_fusion
  1052.3 0.0 copy-start
  1052.3 1.5 copy-done
  1053.8 0.8 slice_dynamic-update-slice_fusion.1
  (4 shorter events, 0.1 us)
Async XLA Ops:
  0.0 1.7 slice-start
  3.1 8.3 copy-start.1
  3.1 40.9 %all-to-all-start = ((bf16[4,96,2304]{2,1,0:T(8,128)(2,1)}), bf16[4,96,2304]{2,1,0:T(8,128)(2,1)S(1)}, u32[]{:S(2)}, u32[]{:S(2)}) async-start(bf16[4,96,2304]{2,1,0:T(8,128)(2,1)} %pad_maximum_fusion.1), calls=%async_computation | async-start | bytes 3538944 | tf_op jit(solution)/shard_map/all_to_all | solution.py:318
  7.5 36.5 %collective-permute-start = (bf16[96,2304]{1,0:T(8,128)(2,1)S(1)}, bf16[96,2304]{1,0:T(8,128)(2,1)S(1)}, u32[]{:S(2)}, u32[]{:S(2)}) collective-permute-start(bf16[96,2304]{1,0:T(8,128)(2,1)S(1)} %get-tuple-element.9), channel_id=1, source_target_pairs={{0,2},{1,0},{2,3},{3,1},{4,6},{5,4},{6,7},{7,5}} | collective-permute-start | bytes 1327112 | tf_op jit(solution)/shard_map/ppermute | solution.py:321
  7.5 36.5 %collective-permute-start.1 = (bf16[96,2304]{1,0:T(8,128)(2,1)S(1)}, bf16[96,2304]{1,0:T(8,128)(2,1)S(1)}, u32[]{:S(2)}, u32[]{:S(2)}) collective-permute-start(bf16[96,2304]{1,0:T(8,128)(2,1)S(1)} %get-tuple-element.10), channel_id=1, source_target_pairs={{0,0},{1,2},{2,1},{3,3},{4,4},{5,6},{6,5},{7,7}} | collective-permute-start | bytes 1327112 | tf_op jit(solution)/shard_map/ppermute | solution.py:320
  1017.7 24.6 %all-to-all-start.1 = ((bf16[4,96,2304]{2,1,0:T(8,128)(2,1)}), bf16[4,96,2304]{2,1,0:T(8,128)(2,1)S(1)}, u32[]{:S(2)}, u32[]{:S(2)}) async-start(bf16[4,96,2304]{2,1,0:T(8,128)(2,1)} %bitcast.7), calls=%async_computation.1 | async-start | bytes 3538944 | tf_op jit(solution)/shard_map/all_to_all | solution.py:328
  1022.5 23.0 %collective-permute-start.3 = (bf16[96,2304]{1,0:T(8,128)(2,1)S(1)}, bf16[96,2304]{1,0:T(8,128)(2,1)S(1)}, u32[]{:S(2)}, u32[]{:S(2)}) collective-permute-start(bf16[96,2304]{1,0:T(8,128)(2,1)S(1)} %get-tuple-element.5), channel_id=1, source_target_pairs={{2,0},{0,1},{3,2},{1,3},{6,4},{4,5},{7,6},{5,7}} | collective-permute-start | bytes 1327112 | tf_op jit(solution)/shard_map/ppermute | solution.py:332
  1023.9 28.1 %collective-permute-start.2 = (bf16[96,2304]{1,0:T(8,128)(2,1)S(1)}, bf16[96,2304]{1,0:T(8,128)(2,1)S(1)}, u32[]{:S(2)}, u32[]{:S(2)}) collective-permute-start(bf16[96,2304]{1,0:T(8,128)(2,1)S(1)} %get-tuple-element.6), channel_id=1, source_target_pairs={{0,0},{2,1},{1,2},{3,3},{4,4},{6,5},{5,6},{7,7}} | collective-permute-start | bytes 1327112 | tf_op jit(solution)/shard_map/ppermute | solution.py:331
  1052.3 1.5 copy-start
